TPU v7x, 32 devices: a whole 2x2x4 slice. The times are simulated.
32 devices in a mesh: py: 4 (over y, core), pz: 8 (over z, x).
Axes of the slice: x: 2, y: 2, z: 4, core: 2. Of those that a mesh axis runs over, the one named last changes fastest.
Arguments:
- wavefunctions: float32 [2, 8, 128, 128, 128], P(None, None, 'pz', 'py'), may hold values from -6 to 6
- potential: float32 [128, 128, 128], P('pz', 'py'), may hold values from -4 to 4
- cutoff_sq: int32 [1], replicated, may hold values from 2304 to 4096
- locked_mask: int32 [8], replicated, may hold values 0 or 1
Outputs:
- applied: float32 [2, 8, 128, 128, 128], P(None, None, 'pz', 'py')
- rayleigh: float32 [8], replicated
- residual_norm: float32 [8], replicated
All inputs are finite; a program needn't handle non-finite values.
Results may differ from a plain program's by a relative error of at most 0.00005.
Values sent between devices are 32-bit elements; how exact they have to be, the bound alone decides.
A program may use at most 64 MiB of HBM per device.

v0:
```python
import math
import jax
import jax.numpy as jnp
from jax import lax
from jax.sharding import PartitionSpec as P


def make_tables(length, inverse):
    counter = jnp.arange(length, dtype=jnp.int32)
    phase = counter[:, None] * counter[None, :] % length
    angle = 2.0 * math.pi / length * phase.astype(jnp.float32)
    if inverse:
        return (jnp.cos(angle) / length, jnp.sin(angle) / length)
    return (jnp.cos(angle), -jnp.sin(angle))


def transform_axis(field, axis, tables):
    cosines, sines = tables
    letters = "abcdefgh"[: field.ndim - 1]
    place = axis - 1
    source = letters[:place] + "n" + letters[place + 1 :]
    target = letters[:place] + "k" + letters[place + 1 :]
    form = source + ",kn->" + target
    real_part = field[0]
    imag_part = field[1]
    high = lax.Precision.HIGHEST
    out_real = jnp.einsum(form, real_part, cosines, precision=high) - jnp.einsum(
        form, imag_part, sines, precision=high
    )
    out_imag = jnp.einsum(form, real_part, sines, precision=high) + jnp.einsum(
        form, imag_part, cosines, precision=high
    )
    return jnp.stack([out_real, out_imag])


def signed_square(counter, length):
    signed = jnp.where(counter < length // 2, counter, counter - length)
    return signed * signed


def kinetic_table(first_sq, second_sq, third_sq, cutoff_sq, length):
    total = first_sq[:, None, None] + second_sq[None, :, None] + third_sq[None, None, :]
    keep = (total <= cutoff_sq[0]).astype(jnp.float32)
    return 0.5 * (math.pi / length) ** 2 * total.astype(jnp.float32) * keep


def slab_kinetic(field, cutoff_sq, forward, inverse):
    parts, bands, rows_z, rows_y, length = field.shape
    size_y = lax.axis_size("py")
    size_z = lax.axis_size("pz")
    along_x = transform_axis(field, 4, forward)
    flat = jnp.moveaxis(along_x, 1, 3).reshape(parts, rows_z, rows_y, bands * length)
    planes = lax.all_to_all(
        lax.all_to_all(flat, "py", split_axis=3, concat_axis=2, tiled=True),
        "pz",
        split_axis=3,
        concat_axis=1,
        tiled=True,
    )
    width = planes.shape[3]
    start = lax.axis_index("py") * (bands * length // size_y) + lax.axis_index("pz") * width
    column = start + jnp.arange(width, dtype=jnp.int32)
    full_counter = jnp.arange(length, dtype=jnp.int32)
    full_sq = signed_square(full_counter, length)
    kinetic = kinetic_table(
        full_sq, full_sq, signed_square(column % length, length), cutoff_sq, length
    )
    spectrum = transform_axis(transform_axis(planes, 1, forward), 2, forward) * kinetic
    spatial = transform_axis(transform_axis(spectrum, 2, inverse), 1, inverse)
    returned = lax.all_to_all(
        lax.all_to_all(spatial, "py", split_axis=2, concat_axis=3, tiled=True),
        "pz",
        split_axis=1,
        concat_axis=3,
        tiled=True,
    )
    ordered = returned.reshape(parts, rows_z, rows_y, size_z, size_y, width)
    ordered = jnp.swapaxes(ordered, 3, 4).reshape(parts, rows_z, rows_y, bands, length)
    return transform_axis(jnp.moveaxis(ordered, 3, 1), 4, inverse)


def apply_kinetic(field, cutoff_sq, forward, inverse):
    return slab_kinetic(field, cutoff_sq, forward, inverse)


def body(wavefunctions, potential, cutoff_sq, locked_mask):
    length = wavefunctions.shape[4]
    forward = make_tables(length, False)
    inverse = make_tables(length, True)
    blocks = wavefunctions.shape[1] // 4

    def one_block(block, result):
        piece = lax.dynamic_slice_in_dim(wavefunctions, block * 4, 4, 1)
        done = apply_kinetic(piece, cutoff_sq, forward, inverse)
        return lax.dynamic_update_slice_in_dim(result, done, block * 4, 1)

    kinetic_part = lax.fori_loop(0, blocks, one_block, jnp.zeros_like(wavefunctions))
    applied = kinetic_part + potential[None, None] * wavefunctions
    norm_local = jnp.sum(wavefunctions * wavefunctions, axis=(0, 2, 3, 4))
    correlation_local = jnp.sum(wavefunctions * applied, axis=(0, 2, 3, 4))
    norm_sq, correlation = lax.psum((norm_local, correlation_local), ("py", "pz"))
    rayleigh = correlation / norm_sq
    residual = applied - rayleigh[None, :, None, None, None] * wavefunctions
    residual_sq = lax.psum(jnp.sum(residual * residual, axis=(0, 2, 3, 4)), ("py", "pz"))
    residual_norm = jnp.sqrt(residual_sq / norm_sq) * (1.0 - locked_mask.astype(jnp.float32))
    return (applied, rayleigh, residual_norm)


def solution(mesh):
    in_specs = (P(None, None, "pz", "py", None), P("pz", "py", None), P(), P())
    out_specs = (P(None, None, "pz", "py", None), P(), P())
    return jax.shard_map(body, mesh=mesh, in_specs=in_specs, out_specs=out_specs, check_vma=False)
```

profile of v0, /device:TPU:0, one launch (start us, length us, event | category | flops | bytes accessed | tf_op | source)
XLA Modules:
  0.0 693.6 jit_solution(16688748125790381216)
XLA Ops:
  0.6 2.5 broadcast_in_dim.14
  3.2 599.9 %while.18 = (s32[]{:T(128)}, f32[2,8,16,32,128]{4,3,2,1,0:T(8,128)}, f32[2,8,16,32,128]{4,3,2,1,0:T(8,128)}, s32[1]{0:T(128)}, s32[]{:T(128)}, /*index=5*/s32[]{...) while((s32[]{:T(128)}, ...), condition=%wide.region_1.2_spmd.clone.clone, body=%wide.region_0.1_spmd.clone.clone.sunk | while | flops 9676570624 | bytes 232916592 | solution.py:97
  3.2 2.5 fusion.346
  8.1 2.5 fusion.347
  10.6 2.5 fusion.345
  13.3 7.5 %copy.142 = f32[2,16,32,4,128]{2,1,0,4,3:T(8,128)} copy(f32[2,16,32,4,128]{4,2,1,3,0:T(8,128)S(1)} %maximum_bitcast_fusion.2) | data formatting | bytes 4194304 | tf_op jit(solution)/shard_map/while/body/eval_jaxpr/reshape | solution.py:52
  20.7 6.1 reshape.143
  26.9 30.2 %all_to_all.204 = f32[4,1,131072]{2,1,0:T(1,128)} all-to-all(f32[4,1,131072]{2,1,0:T(1,128)S(1)} %reshape.143), channel_id=1, replica_groups=mesh['py'=4,'pz'=8] {'py'}, dimensions={0} | all-to-all | bytes 4194304 | tf_op jit(solution)/shard_map/while/body/eval_jaxpr/all_to_all | solution.py:54
  57.6 7.7 %reduce.4 = f32[4,131072]{1,0:T(4,128)S(1)} reduce(f32[4,1,131072]{2,1,0:T(1,128)} %all_to_all.204, f32[]{:T(128)} %broadcast.656), dimensions={1}, to_apply=%all_to_all.178.reduce_sub_computation | reduce | bytes 4194308 | tf_op jit(solution)/shard_map/while/body/eval_jaxpr/all_to_all | solution.py:54
  65.3 6.1 reshape.144
  71.4 5.2 copy.143
  78.2 3.1 copy.145
  81.3 6.9 all-to-all-start.1
  89.3 46.3 %all-to-all-done.1 = f32[2,16,128,128]{2,1,0,3:T(8,128)S(1)} async-done(((f32[2,16,128,128]{2,1,0,3:T(8,128)}), f32[2,16,128,128]{2,1,0,3:T(8,128)S(1)}, u32[]{:S(2)}, u32[]{:S(2)}) %all-to-all-start.1) | async-done | bytes 2097184 | tf_op jit(solution)/shard_map/while/body/eval_jaxpr/all_to_all | solution.py:53
  170.9 28.1 %all_to_all.205 = f32[2,128,128,16]{1,3,0,2:T(8,128)S(1)} all-to-all(f32[2,128,128,16]{1,3,0,2:T(8,128)S(1)} %copy.151), channel_id=1, replica_groups=mesh['py'=4,'pz'=8] {'py'}, dimensions={2} | all-to-all | bytes 4194304 | tf_op jit(solution)/shard_map/while/body/eval_jaxpr/all_to_all | solution.py:71
  199.3 4.5 copy.153
  203.8 7.2 %reshape.145 = f32[8,1,65536]{2,1,0:T(1,128)} reshape(f32[128,2,32,64]{3,2,1,0:T(8,128)} %bitcast.327) | data formatting | bytes 4194304 | tf_op jit(solution)/shard_map/while
  211.0 3.9 all-to-all-start.3
  214.9 48.0 %all-to-all-done.3 = f32[8,1,65536]{2,1,0:T(1,128)S(1)} async-done(((f32[8,1,65536]{2,1,0:T(1,128)}), f32[8,1,65536]{2,1,0:T(1,128)S(1)}, u32[]{:S(2)}, u32[]{:S(2)}) %all-to-all-start.3) | async-done | bytes 2097184 | tf_op jit(solution)/shard_map/while/body/eval_jaxpr/all_to_all | solution.py:70
  264.8 7.2 %reduce.5 = f32[8,65536]{1,0:T(8,128)S(1)} reduce(f32[8,1,65536]{2,1,0:T(1,128)} %copy-done, f32[]{:T(128)} %broadcast.657), dimensions={1}, to_apply=%all_to_all.189.reduce_sub_computation | reduce | bytes 4194308 | tf_op jit(solution)/shard_map/while/body/eval_jaxpr/all_to_all | solution.py:70
  272.0 3.6 reshape.146
  275.6 7.0 %copy.154 = f32[2,16,32,8,64]{2,4,3,1,0:T(8,128)} copy(f32[2,16,32,8,64]{4,2,0,1,3:T(8,128)} %bitcast.326) | data formatting | bytes 4194304 | tf_op jit(solution)/shard_map/while/body/eval_jaxpr/all_to_all | solution.py:70
  282.6 7.9 %copy.155 = f32[2,16,32,4,8,16]{2,5,4,3,1,0:T(8,128)} copy(f32[2,16,32,4,8,16]{2,5,3,4,1,0:T(8,128)} %bitcast.320) | data formatting | bytes 4194304 | tf_op jit(solution)/shard_map/while/body/eval_jaxpr/transpose | solution.py:78
  290.5 5.6 copy.156
  308.4 2.5 fusion.347
  313.5 7.5 %copy.142 = f32[2,16,32,4,128]{2,1,0,4,3:T(8,128)} copy(f32[2,16,32,4,128]{4,2,1,3,0:T(8,128)S(1)} %maximum_bitcast_fusion.2) | data formatting | bytes 4194304 | tf_op jit(solution)/shard_map/while/body/eval_jaxpr/reshape | solution.py:52
  321.0 6.1 reshape.143
  327.2 29.1 %all_to_all.204 = f32[4,1,131072]{2,1,0:T(1,128)} all-to-all(f32[4,1,131072]{2,1,0:T(1,128)S(1)} %reshape.143), channel_id=1, replica_groups=mesh['py'=4,'pz'=8] {'py'}, dimensions={0} | all-to-all | bytes 4194304 | tf_op jit(solution)/shard_map/while/body/eval_jaxpr/all_to_all | solution.py:54
  356.8 7.7 %reduce.4 = f32[4,131072]{1,0:T(4,128)S(1)} reduce(f32[4,1,131072]{2,1,0:T(1,128)} %all_to_all.204, f32[]{:T(128)} %broadcast.656), dimensions={1}, to_apply=%all_to_all.178.reduce_sub_computation | reduce | bytes 4194308 | tf_op jit(solution)/shard_map/while/body/eval_jaxpr/all_to_all | solution.py:54
  364.5 6.1 reshape.144
  370.6 5.2 copy.143
  377.5 3.1 copy.145
  380.5 4.0 all-to-all-start.1
  385.6 46.7 %all-to-all-done.1 = f32[2,16,128,128]{2,1,0,3:T(8,128)S(1)} async-done(((f32[2,16,128,128]{2,1,0,3:T(8,128)}), f32[2,16,128,128]{2,1,0,3:T(8,128)S(1)}, u32[]{:S(2)}, u32[]{:S(2)}) %all-to-all-start.1) | async-done | bytes 2097184 | tf_op jit(solution)/shard_map/while/body/eval_jaxpr/all_to_all | solution.py:53
  467.6 28.1 %all_to_all.205 = f32[2,128,128,16]{1,3,0,2:T(8,128)S(1)} all-to-all(f32[2,128,128,16]{1,3,0,2:T(8,128)S(1)} %copy.151), channel_id=1, replica_groups=mesh['py'=4,'pz'=8] {'py'}, dimensions={2} | all-to-all | bytes 4194304 | tf_op jit(solution)/shard_map/while/body/eval_jaxpr/all_to_all | solution.py:71
  496.0 4.5 copy.153
  500.5 7.2 %reshape.145 = f32[8,1,65536]{2,1,0:T(1,128)} reshape(f32[128,2,32,64]{3,2,1,0:T(8,128)} %bitcast.327) | data formatting | bytes 4194304 | tf_op jit(solution)/shard_map/while
  507.7 3.9 all-to-all-start.3
  511.6 48.0 %all-to-all-done.3 = f32[8,1,65536]{2,1,0:T(1,128)S(1)} async-done(((f32[8,1,65536]{2,1,0:T(1,128)}), f32[8,1,65536]{2,1,0:T(1,128)S(1)}, u32[]{:S(2)}, u32[]{:S(2)}) %all-to-all-start.3) | async-done | bytes 2097184 | tf_op jit(solution)/shard_map/while/body/eval_jaxpr/all_to_all | solution.py:70
  561.5 7.2 %reduce.5 = f32[8,65536]{1,0:T(8,128)S(1)} reduce(f32[8,1,65536]{2,1,0:T(1,128)} %copy-done, f32[]{:T(128)} %broadcast.657), dimensions={1}, to_apply=%all_to_all.189.reduce_sub_computation | reduce | bytes 4194308 | tf_op jit(solution)/shard_map/while/body/eval_jaxpr/all_to_all | solution.py:70
  568.7 3.6 reshape.146
  572.3 7.0 %copy.154 = f32[2,16,32,8,64]{2,4,3,1,0:T(8,128)} copy(f32[2,16,32,8,64]{4,2,0,1,3:T(8,128)} %bitcast.326) | data formatting | bytes 4194304 | tf_op jit(solution)/shard_map/while/body/eval_jaxpr/all_to_all | solution.py:70
  579.3 7.9 %copy.155 = f32[2,16,32,4,8,16]{2,5,4,3,1,0:T(8,128)} copy(f32[2,16,32,4,8,16]{2,5,3,4,1,0:T(8,128)} %bitcast.320) | data formatting | bytes 4194304 | tf_op jit(solution)/shard_map/while/body/eval_jaxpr/transpose | solution.py:78
  587.2 5.6 copy.156
  603.1 6.5 multiply_reduce_fusion.1
  609.6 37.5 %all-reduce = (f32[8]{0:T(128)S(1)}, f32[8]{0:T(128)S(1)}) all-reduce(f32[8]{0:T(128)S(1)} %get-tuple-element.349, f32[8]{0:T(128)S(1)} %get-tuple-element.348), channel_id=1, replica_groups=mesh['py'=4,'pz'=8] {'py','pz'}, use_global_device_ids=true, to_apply=%region_3.4 | all-reduce | flops 16 | bytes 128 | tf_op jit(solution)/shard_map/psum | solution.py:101
  647.2 4.2 multiply_reduce_fusion
  651.4 41.5 %psum.23 = f32[8]{0:T(128)S(1)} all-reduce(f32[8]{0:T(128)S(1)} %multiply_reduce_fusion), channel_id=1, replica_groups=mesh['py'=4,'pz'=8] {'py','pz'}, use_global_device_ids=true, to_apply=%region_7.8 | all-reduce | flops 8 | bytes 64 | tf_op jit(solution)/shard_map/psum | solution.py:104
  (106 shorter events, 105.8 us)
Async XLA Ops:
  3.2 599.9 %copy-start.4 = (f32[16,32,128]{2,1,0:T(8,128)S(1)}, f32[16,32,128]{2,1,0:T(8,128)}, u32[]{:S(2)}) copy-start(f32[16,32,128]{2,1,0:T(8,128)} %param.7) | copy-start | bytes 786436
  81.3 54.2 %all-to-all-start.1 = ((f32[2,16,128,128]{2,1,0,3:T(8,128)}), f32[2,16,128,128]{2,1,0,3:T(8,128)S(1)}, u32[]{:S(2)}, u32[]{:S(2)}) async-start(f32[2,16,128,128]{2,1,0,3:T(8,128)} %copy.145), calls=%async_computation.1 | async-start | bytes 4194304 | tf_op jit(solution)/shard_map/while/body/eval_jaxpr/all_to_all | solution.py:53
  138.5 3.5 copy-start.1
  211.0 51.9 %all-to-all-start.3 = ((f32[8,1,65536]{2,1,0:T(1,128)}), f32[8,1,65536]{2,1,0:T(1,128)S(1)}, u32[]{:S(2)}, u32[]{:S(2)}) async-start(f32[8,1,65536]{2,1,0:T(1,128)} %reshape.145), calls=%async_computation.3 | async-start | bytes 4194304 | tf_op jit(solution)/shard_map/while/body/eval_jaxpr/all_to_all | solution.py:70
  262.9 1.4 copy-start
  298.6 2.5 copy-start.2
  301.3 2.0 copy-start.3
  380.5 51.7 %all-to-all-start.1 = ((f32[2,16,128,128]{2,1,0,3:T(8,128)}), f32[2,16,128,128]{2,1,0,3:T(8,128)S(1)}, u32[]{:S(2)}, u32[]{:S(2)}) async-start(f32[2,16,128,128]{2,1,0,3:T(8,128)} %copy.145), calls=%async_computation.1 | async-start | bytes 4194304 | tf_op jit(solution)/shard_map/while/body/eval_jaxpr/all_to_all | solution.py:53
  435.2 3.5 copy-start.1
  507.7 51.9 %all-to-all-start.3 = ((f32[8,1,65536]{2,1,0:T(1,128)}), f32[8,1,65536]{2,1,0:T(1,128)S(1)}, u32[]{:S(2)}, u32[]{:S(2)}) async-start(f32[8,1,65536]{2,1,0:T(1,128)} %reshape.145), calls=%async_computation.3 | async-start | bytes 4194304 | tf_op jit(solution)/shard_map/while/body/eval_jaxpr/all_to_all | solution.py:70
  559.6 1.4 copy-start
  595.2 2.5 copy-start.2
  598.0 2.0 copy-start.3
  647.1 4.2 copy-start.5
  647.2 45.7 %copy-start.6 = (s32[8]{0:T(128)S(1)}, s32[8]{0:T(128)}, u32[]{:S(2)}) copy-start(s32[8]{0:T(128)} %param.9) | copy-start | bytes 100
where the time goes:
time: 697 us; the launch traced here: 694 us
  blocking collectives  195 us (28%)
  waiting for transfers between devices  189 us (27%)
  local copies, waits for them, and re-layouts  156 us (22%)
  matrix products  85.4 us (12%)
  other arithmetic  44.8 us (6%)
  starting transfers between devices  18.7 us (3%)
    all_to_all x2, waiting for transfers between devices, slab_kinetic(): lax.all_to_all(lax.all_to_all(spatial, 'py', split_axis=2, concat_axis=3,...  96 us
    all_to_all x2, waiting for transfers between devices, slab_kinetic(): lax.all_to_all(lax.all_to_all(flat, 'py', split_axis=3, concat_axis=2, ti...  92.9 us
    all_to_all x2, blocking collectives, slab_kinetic(): lax.all_to_all(flat, 'py', split_axis=3, concat_axis=2, tiled=True)  59.3 us
    all_to_all x2, blocking collectives, slab_kinetic(): lax.all_to_all(spatial, 'py', split_axis=2, concat_axis=3, tiled=True)  56.3 us
    while x24, local copies, waits for them, and re-layouts  52.9 us
    psum x1, blocking collectives, body(): lax.psum(jnp.sum(residual * residual, axis=(0, 2, 3, 4)), ('py', 'pz'))  41.5 us
    psum x1, blocking collectives, body(): lax.psum((norm_local, correlation_local), ('py', 'pz'))  37.5 us
    dot_general x12, matrix products, transform_axis(): jnp.einsum(form, imag_part, sines, precision=high)  22.5 us
  transfers between devices with their start and end apart: 4, of which 4 were waited for; matrix products, arithmetic and copies ran while one was open for 0% of the time, Pallas kernels for 0%

commit v1 on v0

--- a/solution.py
+++ b/solution.py
@@ -3,6 +3,11 @@
 import jax.numpy as jnp
 from jax import lax
 from jax.sharding import PartitionSpec as P
+
+
+def by_each_axis(array, first, second):
+    inner = lax.psum(array, first)
+    return lax.psum(inner, second)
 
 
 def make_tables(length, inverse):
@@ -98,7 +103,7 @@
     applied = kinetic_part + potential[None, None] * wavefunctions
     norm_local = jnp.sum(wavefunctions * wavefunctions, axis=(0, 2, 3, 4))
     correlation_local = jnp.sum(wavefunctions * applied, axis=(0, 2, 3, 4))
-    norm_sq, correlation = lax.psum((norm_local, correlation_local), ("py", "pz"))
+    norm_sq, correlation = by_each_axis((norm_local, correlation_local), "pz", "py")
     rayleigh = correlation / norm_sq
     residual = applied - rayleigh[None, :, None, None, None] * wavefunctions
     residual_sq = lax.psum(jnp.sum(residual * residual, axis=(0, 2, 3, 4)), ("py", "pz"))

time: 697 us -> 680 us (0.976)
  blocking collectives: 195 us -> 178 us
    psum x1 -> x2, blocking collectives: 37.5 us -> 25.1 us  [the longest x1 19.4 us: by_each_axis(): inner = lax.psum(array, first)]
where the time goes in v1:
time: 680 us; the launch traced here: 676 us
  waiting for transfers between devices  189 us (28%)
  blocking collectives  178 us (26%)
  local copies, waits for them, and re-layouts  156 us (23%)
  matrix products  85.4 us (13%)
  other arithmetic  44.8 us (7%)
  starting transfers between devices  18.7 us (3%)
    all_to_all x2, waiting for transfers between devices, slab_kinetic(): lax.all_to_all(lax.all_to_all(spatial, 'py', split_axis=2, concat_axis=3,...  96 us
    all_to_all x2, waiting for transfers between devices, slab_kinetic(): lax.all_to_all(lax.all_to_all(flat, 'py', split_axis=3, concat_axis=2, ti...  92.9 us
    all_to_all x2, blocking collectives, slab_kinetic(): lax.all_to_all(flat, 'py', split_axis=3, concat_axis=2, tiled=True)  59.3 us
    all_to_all x2, blocking collectives, slab_kinetic(): lax.all_to_all(spatial, 'py', split_axis=2, concat_axis=3, tiled=True)  56.3 us
    while x24, local copies, waits for them, and re-layouts  52.9 us
    psum x1, blocking collectives, body(): lax.psum(jnp.sum(residual * residual, axis=(0, 2, 3, 4)), ('py', 'pz'))  36.9 us
    dot_general x12, matrix products, transform_axis(): jnp.einsum(form, imag_part, sines, precision=high)  22.5 us
    dot_general x12, matrix products, transform_axis(): jnp.einsum(form, real_part, cosines, precision=high)  22 us
  transfers between devices with their start and end apart: 4, of which 4 were waited for; matrix products, arithmetic and copies ran while one was open for 0% of the time, Pallas kernels for 0%

profile of v1, /device:TPU:0, one launch (start us, length us, event | category | flops | bytes accessed | tf_op | source)
XLA Modules:
  0.0 676.3 jit_solution(3179466376171270911)
XLA Ops:
  0.6 2.5 broadcast_in_dim.14
  3.2 599.6 %while.18 = (s32[]{:T(128)}, f32[2,8,16,32,128]{4,3,2,1,0:T(8,128)}, f32[2,8,16,32,128]{4,3,2,1,0:T(8,128)}, s32[1]{0:T(128)}, s32[]{:T(128)}, /*index=5*/s32[]{...) while((s32[]{:T(128)}, ...), condition=%wide.region_1.2_spmd.clone.clone, body=%wide.region_0.1_spmd.clone.clone.sunk | while | flops 9676570624 | bytes 232916592 | solution.py:102
  3.2 2.5 fusion.346
  8.1 2.5 fusion.347
  13.3 7.5 %copy.142 = f32[2,16,32,4,128]{2,1,0,4,3:T(8,128)} copy(f32[2,16,32,4,128]{4,2,1,3,0:T(8,128)S(1)} %maximum_bitcast_fusion.2) | data formatting | bytes 4194304 | tf_op jit(solution)/shard_map/while/body/eval_jaxpr/reshape | solution.py:57
  20.7 6.1 reshape.143
  26.9 30.2 %all_to_all.204 = f32[4,1,131072]{2,1,0:T(1,128)} all-to-all(f32[4,1,131072]{2,1,0:T(1,128)S(1)} %reshape.143), channel_id=1, replica_groups=mesh['py'=4,'pz'=8] {'py'}, dimensions={0} | all-to-all | bytes 4194304 | tf_op jit(solution)/shard_map/while/body/eval_jaxpr/all_to_all | solution.py:59
  57.6 7.7 %reduce.4 = f32[4,131072]{1,0:T(4,128)S(1)} reduce(f32[4,1,131072]{2,1,0:T(1,128)} %all_to_all.204, f32[]{:T(128)} %broadcast.656), dimensions={1}, to_apply=%all_to_all.178.reduce_sub_computation | reduce | bytes 4194308 | tf_op jit(solution)/shard_map/while/body/eval_jaxpr/all_to_all | solution.py:59
  65.3 6.1 reshape.144
  71.4 5.2 copy.143
  78.2 3.1 copy.145
  81.3 6.9 %all-to-all-start.1 = ((f32[2,16,128,128]{2,1,0,3:T(8,128)}), f32[2,16,128,128]{2,1,0,3:T(8,128)S(1)}, u32[]{:S(2)}, u32[]{:S(2)}) async-start(f32[2,16,128,128]{2,1,0,3:T(8,128)} %copy.145), calls=%async_computation.1 | async-start | bytes 4194304 | tf_op jit(solution)/shard_map/while/body/eval_jaxpr/all_to_all | solution.py:58
  89.3 46.3 %all-to-all-done.1 = f32[2,16,128,128]{2,1,0,3:T(8,128)S(1)} async-done(((f32[2,16,128,128]{2,1,0,3:T(8,128)}), f32[2,16,128,128]{2,1,0,3:T(8,128)S(1)}, u32[]{:S(2)}, u32[]{:S(2)}) %all-to-all-start.1) | async-done | bytes 2097184 | tf_op jit(solution)/shard_map/while/body/eval_jaxpr/all_to_all | solution.py:58
  170.9 28.1 %all_to_all.205 = f32[2,128,128,16]{1,3,0,2:T(8,128)S(1)} all-to-all(f32[2,128,128,16]{1,3,0,2:T(8,128)S(1)} %copy.151), channel_id=1, replica_groups=mesh['py'=4,'pz'=8] {'py'}, dimensions={2} | all-to-all | bytes 4194304 | tf_op jit(solution)/shard_map/while/body/eval_jaxpr/all_to_all | solution.py:76
  199.3 4.5 copy.153
  203.8 7.2 %reshape.145 = f32[8,1,65536]{2,1,0:T(1,128)} reshape(f32[128,2,32,64]{3,2,1,0:T(8,128)} %bitcast.327) | data formatting | bytes 4194304 | tf_op jit(solution)/shard_map/while
  211.0 3.9 all-to-all-start.3
  214.9 48.0 %all-to-all-done.3 = f32[8,1,65536]{2,1,0:T(1,128)S(1)} async-done(((f32[8,1,65536]{2,1,0:T(1,128)}), f32[8,1,65536]{2,1,0:T(1,128)S(1)}, u32[]{:S(2)}, u32[]{:S(2)}) %all-to-all-start.3) | async-done | bytes 2097184 | tf_op jit(solution)/shard_map/while/body/eval_jaxpr/all_to_all | solution.py:75
  264.8 7.2 %reduce.5 = f32[8,65536]{1,0:T(8,128)S(1)} reduce(f32[8,1,65536]{2,1,0:T(1,128)} %copy-done, f32[]{:T(128)} %broadcast.657), dimensions={1}, to_apply=%all_to_all.189.reduce_sub_computation | reduce | bytes 4194308 | tf_op jit(solution)/shard_map/while/body/eval_jaxpr/all_to_all | solution.py:75
  272.0 3.6 reshape.146
  275.6 7.0 %copy.154 = f32[2,16,32,8,64]{2,4,3,1,0:T(8,128)} copy(f32[2,16,32,8,64]{4,2,0,1,3:T(8,128)} %bitcast.326) | data formatting | bytes 4194304 | tf_op jit(solution)/shard_map/while/body/eval_jaxpr/all_to_all | solution.py:75
  282.6 7.9 %copy.155 = f32[2,16,32,4,8,16]{2,5,4,3,1,0:T(8,128)} copy(f32[2,16,32,4,8,16]{2,5,3,4,1,0:T(8,128)} %bitcast.320) | data formatting | bytes 4194304 | tf_op jit(solution)/shard_map/while/body/eval_jaxpr/transpose | solution.py:83
  290.5 5.6 copy.156
  308.4 2.5 fusion.347
  313.5 7.5 %copy.142 = f32[2,16,32,4,128]{2,1,0,4,3:T(8,128)} copy(f32[2,16,32,4,128]{4,2,1,3,0:T(8,128)S(1)} %maximum_bitcast_fusion.2) | data formatting | bytes 4194304 | tf_op jit(solution)/shard_map/while/body/eval_jaxpr/reshape | solution.py:57
  321.0 6.1 reshape.143
  327.2 29.1 %all_to_all.204 = f32[4,1,131072]{2,1,0:T(1,128)} all-to-all(f32[4,1,131072]{2,1,0:T(1,128)S(1)} %reshape.143), channel_id=1, replica_groups=mesh['py'=4,'pz'=8] {'py'}, dimensions={0} | all-to-all | bytes 4194304 | tf_op jit(solution)/shard_map/while/body/eval_jaxpr/all_to_all | solution.py:59
  356.8 7.7 %reduce.4 = f32[4,131072]{1,0:T(4,128)S(1)} reduce(f32[4,1,131072]{2,1,0:T(1,128)} %all_to_all.204, f32[]{:T(128)} %broadcast.656), dimensions={1}, to_apply=%all_to_all.178.reduce_sub_computation | reduce | bytes 4194308 | tf_op jit(solution)/shard_map/while/body/eval_jaxpr/all_to_all | solution.py:59
  364.5 6.1 reshape.144
  370.6 5.2 copy.143
  377.5 3.1 copy.145
  380.5 4.0 all-to-all-start.1
  385.6 46.7 %all-to-all-done.1 = f32[2,16,128,128]{2,1,0,3:T(8,128)S(1)} async-done(((f32[2,16,128,128]{2,1,0,3:T(8,128)}), f32[2,16,128,128]{2,1,0,3:T(8,128)S(1)}, u32[]{:S(2)}, u32[]{:S(2)}) %all-to-all-start.1) | async-done | bytes 2097184 | tf_op jit(solution)/shard_map/while/body/eval_jaxpr/all_to_all | solution.py:58
  467.6 28.1 %all_to_all.205 = f32[2,128,128,16]{1,3,0,2:T(8,128)S(1)} all-to-all(f32[2,128,128,16]{1,3,0,2:T(8,128)S(1)} %copy.151), channel_id=1, replica_groups=mesh['py'=4,'pz'=8] {'py'}, dimensions={2} | all-to-all | bytes 4194304 | tf_op jit(solution)/shard_map/while/body/eval_jaxpr/all_to_all | solution.py:76
  496.0 4.5 copy.153
  500.5 7.2 %reshape.145 = f32[8,1,65536]{2,1,0:T(1,128)} reshape(f32[128,2,32,64]{3,2,1,0:T(8,128)} %bitcast.327) | data formatting | bytes 4194304 | tf_op jit(solution)/shard_map/while
  507.7 3.9 all-to-all-start.3
  511.6 48.0 %all-to-all-done.3 = f32[8,1,65536]{2,1,0:T(1,128)S(1)} async-done(((f32[8,1,65536]{2,1,0:T(1,128)}), f32[8,1,65536]{2,1,0:T(1,128)S(1)}, u32[]{:S(2)}, u32[]{:S(2)}) %all-to-all-start.3) | async-done | bytes 2097184 | tf_op jit(solution)/shard_map/while/body/eval_jaxpr/all_to_all | solution.py:75
  561.5 7.2 %reduce.5 = f32[8,65536]{1,0:T(8,128)S(1)} reduce(f32[8,1,65536]{2,1,0:T(1,128)} %copy-done, f32[]{:T(128)} %broadcast.657), dimensions={1}, to_apply=%all_to_all.189.reduce_sub_computation | reduce | bytes 4194308 | tf_op jit(solution)/shard_map/while/body/eval_jaxpr/all_to_all | solution.py:75
  568.7 3.6 reshape.146
  572.3 7.0 %copy.154 = f32[2,16,32,8,64]{2,4,3,1,0:T(8,128)} copy(f32[2,16,32,8,64]{4,2,0,1,3:T(8,128)} %bitcast.326) | data formatting | bytes 4194304 | tf_op jit(solution)/shard_map/while/body/eval_jaxpr/all_to_all | solution.py:75
  579.3 7.9 %copy.155 = f32[2,16,32,4,8,16]{2,5,4,3,1,0:T(8,128)} copy(f32[2,16,32,4,8,16]{2,5,3,4,1,0:T(8,128)} %bitcast.320) | data formatting | bytes 4194304 | tf_op jit(solution)/shard_map/while/body/eval_jaxpr/transpose | solution.py:83
  587.2 5.6 copy.156
  602.8 6.5 multiply_reduce_fusion.1
  609.3 19.4 %all-reduce = (f32[8]{0:T(128)S(1)}, f32[8]{0:T(128)S(1)}) all-reduce(f32[8]{0:T(128)S(1)} %get-tuple-element.349, f32[8]{0:T(128)S(1)} %get-tuple-element.348), channel_id=1, replica_groups=mesh['py'=4,'pz'=8] {'pz'}, use_global_device_ids=true, to_apply=%region_3.4 | all-reduce | flops 16 | bytes 128 | tf_op jit(solution)/shard_map/psum | solution.py:9
  628.8 5.6 all-reduce.1
  634.4 4.2 multiply_reduce_fusion
  638.7 36.9 %psum.39 = f32[8]{0:T(128)S(1)} all-reduce(f32[8]{0:T(128)S(1)} %multiply_reduce_fusion), channel_id=1, replica_groups=mesh['py'=4,'pz'=8] {'py','pz'}, use_global_device_ids=true, to_apply=%region_9.10 | all-reduce | flops 8 | bytes 64 | tf_op jit(solution)/shard_map/psum | solution.py:109
  (107 shorter events, 108.3 us)
Async XLA Ops:
  3.2 599.6 %copy-start.4 = (f32[16,32,128]{2,1,0:T(8,128)S(1)}, f32[16,32,128]{2,1,0:T(8,128)}, u32[]{:S(2)}) copy-start(f32[16,32,128]{2,1,0:T(8,128)} %param.7) | copy-start | bytes 786436
  81.3 54.2 %all-to-all-start.1 = ((f32[2,16,128,128]{2,1,0,3:T(8,128)}), f32[2,16,128,128]{2,1,0,3:T(8,128)S(1)}, u32[]{:S(2)}, u32[]{:S(2)}) async-start(f32[2,16,128,128]{2,1,0,3:T(8,128)} %copy.145), calls=%async_computation.1 | async-start | bytes 4194304 | tf_op jit(solution)/shard_map/while/body/eval_jaxpr/all_to_all | solution.py:58
  138.5 3.5 copy-start.1
  211.0 51.9 %all-to-all-start.3 = ((f32[8,1,65536]{2,1,0:T(1,128)}), f32[8,1,65536]{2,1,0:T(1,128)S(1)}, u32[]{:S(2)}, u32[]{:S(2)}) async-start(f32[8,1,65536]{2,1,0:T(1,128)} %reshape.145), calls=%async_computation.3 | async-start | bytes 4194304 | tf_op jit(solution)/shard_map/while/body/eval_jaxpr/all_to_all | solution.py:75
  262.9 1.4 copy-start
  298.6 2.5 copy-start.2
  301.3 2.0 copy-start.3
  380.5 51.7 %all-to-all-start.1 = ((f32[2,16,128,128]{2,1,0,3:T(8,128)}), f32[2,16,128,128]{2,1,0,3:T(8,128)S(1)}, u32[]{:S(2)}, u32[]{:S(2)}) async-start(f32[2,16,128,128]{2,1,0,3:T(8,128)} %copy.145), calls=%async_computation.1 | async-start | bytes 4194304 | tf_op jit(solution)/shard_map/while/body/eval_jaxpr/all_to_all | solution.py:58
  435.2 3.5 copy-start.1
  507.7 51.9 %all-to-all-start.3 = ((f32[8,1,65536]{2,1,0:T(1,128)}), f32[8,1,65536]{2,1,0:T(1,128)S(1)}, u32[]{:S(2)}, u32[]{:S(2)}) async-start(f32[8,1,65536]{2,1,0:T(1,128)} %reshape.145), calls=%async_computation.3 | async-start | bytes 4194304 | tf_op jit(solution)/shard_map/while/body/eval_jaxpr/all_to_all | solution.py:75
  559.6 1.4 copy-start
  595.2 2.5 copy-start.2
  598.0 2.0 copy-start.3
  634.4 4.2 copy-start.5
  634.4 41.1 %copy-start.6 = (s32[8]{0:T(128)S(1)}, s32[8]{0:T(128)}, u32[]{:S(2)}) copy-start(s32[8]{0:T(128)} %param.9) | copy-start | bytes 100
